TPU v7x, 32 devices: a whole 2x2x4 slice. The times are simulated.
32 devices in a mesh: role: 2 (over x), grp: 8 (over z, y), tp: 2 (over core).
Axes of the slice: x: 2, y: 2, z: 4, core: 2. Of those that a mesh axis runs over, the one named last changes fastest.
Arguments:
- q_new: bfloat16 [256, 4096], P('grp', ('role', 'tp')), may hold values from -9 to 9
- k_new: bfloat16 [256, 512], P('grp', ('role', 'tp')), may hold values from -6 to 6
- v_new: bfloat16 [256, 512], P('grp', ('role', 'tp')), may hold values from -6 to 6
- k_cache: bfloat16 [256, 128, 512], P('grp', None, ('role', 'tp')), may hold values from -9 to 9
- v_cache: bfloat16 [256, 128, 512], P('grp', None, ('role', 'tp')), may hold values from -6 to 6
- cache_len: int32 [256], P('grp'), may hold values from 1 to 127
- cycle_start: int32 [256], P('grp'), may hold values from 0 to 127
- residual: bfloat16 [256, 2880], P('grp', ('role', 'tp')), may hold values from -6 to 6
- out_proj: bfloat16 [4096, 2880], P(('role', 'tp')), may hold values from -0.09375 to 0.09375
- norm_gain: float32 [2880], replicated, may hold values from 0.25 to 1.75
- router: bfloat16 [2880, 8], P(('role', 'tp')), may hold values from -0.21875 to 0.21875
- route_ids: int32 [256, 4], P('grp'), may hold values from 0 to 7, all different within a row; in each aligned block of 32 rows (0 to 31, 32 to 63, ...) at most 18 rows name the same one
- w_gate: bfloat16 [8, 2880, 1440], P('grp', None, ('role', 'tp')), may hold values from -0.109375 to 0.109375
- w_up: bfloat16 [8, 2880, 1440], P('grp', None, ('role', 'tp')), may hold values from -0.109375 to 0.109375
- w_down: bfloat16 [8, 1440, 2880], P('grp', ('role', 'tp')), may hold values from -0.15625 to 0.15625
Outputs:
- attended: bfloat16 [256, 2880], P('grp', ('role', 'tp'))
- expert_mix: bfloat16 [256, 2880], P('grp', ('role', 'tp'))
Inputs may be any that keep to these rules, and one draw needn't show every extreme that they name: `route_ids`: the 4 experts of a token differ. Among the tokens of one grp index (aligned blocks of 32 tokens) no expert is named more than 18 times, a bound that some block reaches.
All inputs are finite; a program needn't handle non-finite values.
Results may differ from a plain program's by a relative error of at most 0.017.
Values may be sent and summed in bfloat16 or wider, within the bound.
No kernel may reach another device: no remote copies, remote signals or barrier semaphores. Data moves between devices by JAX's collectives and lax.ppermute only.
A program may use at most 64 MiB of HBM per device.

v0:
```python
import jax
import jax.numpy as jnp
from jax import lax
from jax.sharding import PartitionSpec as P

HEADS = 64
KV_HEADS = 8
HD = 64
epsilon = 1e-05


def attend(q_new, k_new, v_new, k_cache, v_cache, cache_len, cycle_start):
    tokens = q_new.shape[0]
    window = k_cache.shape[1]
    kv_local = k_new.shape[1] // HD
    grouped = HEADS // KV_HEADS
    queries = q_new.reshape(tokens, kv_local, grouped, HD)
    cached_keys = k_cache.reshape(tokens, window, kv_local, HD)
    cached_values = v_cache.reshape(tokens, window, kv_local, HD)
    own_key = k_new.reshape(tokens, kv_local, HD)
    own_value = v_new.reshape(tokens, kv_local, HD)
    factor = HD ** (-0.5)
    scores = (
        jnp.einsum("tkgd,tskd->tkgs", queries, cached_keys, preferred_element_type=jnp.float32)
        * factor
    )
    own_score = (
        jnp.einsum("tkgd,tkd->tkg", queries, own_key, preferred_element_type=jnp.float32) * factor
    )
    positions = jnp.arange(window, dtype=jnp.int32)
    usable = (positions[None, :] - cycle_start[:, None]) % window < cache_len[:, None]
    usable = usable[:, None, None, :]
    masked = jnp.where(usable, scores, -1e30)
    highest = jnp.maximum(jnp.max(masked, axis=3), own_score)
    lifted = jnp.where(usable, jnp.exp(masked - highest[..., None]), 0.0)
    own_lift = jnp.exp(own_score - highest)
    denominator = jnp.sum(lifted, axis=3) + own_lift
    weights = (lifted / denominator[..., None]).astype(jnp.bfloat16)
    own_weight = (own_lift / denominator).astype(jnp.bfloat16)
    combined = jnp.einsum(
        "tkgs,tskd->tkgd", weights, cached_values, preferred_element_type=jnp.float32
    )
    combined = (
        combined
        + own_weight.astype(jnp.float32)[..., None] * own_value.astype(jnp.float32)[:, :, None, :]
    )
    return combined.reshape(tokens, -1).astype(jnp.bfloat16)


def slot_tables(route_ids, logits, capacity):
    experts_count = logits.shape[1]
    named = route_ids[:, :, None] == jnp.arange(experts_count, dtype=jnp.int32)
    chosen = jnp.sum(jnp.where(named, logits[:, None, :], 0.0), axis=2)
    lifted = jnp.exp(chosen)
    route_weight = lifted / jnp.sum(lifted, axis=1, keepdims=True)
    counts = jnp.sum(named.astype(jnp.int32), axis=1)
    earlier = jnp.cumsum(counts, axis=0) - counts
    ranks = jnp.sum(jnp.where(named, earlier[:, None, :], 0), axis=2)
    placed = named[:, :, :, None] & (
        ranks[:, :, None, None] == jnp.arange(capacity, dtype=jnp.int32)
    )
    select = jnp.sum(placed.astype(jnp.float32), axis=1).reshape(route_ids.shape[0], -1)
    mixing = jnp.sum(jnp.where(placed, route_weight[:, :, None, None], 0.0), axis=1).reshape(
        route_ids.shape[0], -1
    )
    return (select, mixing)


def serve(received, w_gate, w_up, w_down):
    sources = received.shape[0]
    items = received.shape[1]
    inputs = received.reshape(sources * items, received.shape[2])
    gate_lin = jnp.dot(inputs, w_gate[0], preferred_element_type=jnp.float32)
    up_lin = jnp.dot(inputs, w_up[0], preferred_element_type=jnp.float32)
    activated = (gate_lin * jax.nn.sigmoid(1.702 * gate_lin) * (up_lin + 1.0)).astype(jnp.bfloat16)
    partial_out = jnp.dot(activated, w_down[0], preferred_element_type=jnp.float32).reshape(
        sources, items, -1
    )
    rounded = lax.optimization_barrier(partial_out.astype(jnp.bfloat16))
    return lax.all_to_all(rounded, "grp", split_axis=0, concat_axis=0, tiled=True)


def local(
    q_new,
    k_new,
    v_new,
    k_cache,
    v_cache,
    cache_len,
    cycle_start,
    residual,
    out_proj,
    norm_gain,
    router,
    route_ids,
    w_gate,
    w_up,
    w_down,
):
    share = lax.axis_index(("role", "tp"))
    quarter = residual.shape[1]
    heads_out = attend(q_new, k_new, v_new, k_cache, v_cache, cache_len, cycle_start)
    projected = jnp.dot(heads_out, out_proj, preferred_element_type=jnp.float32)
    stream = lax.all_gather(residual, ("role", "tp"), axis=1, tiled=True).astype(
        jnp.float32
    ) + lax.psum(projected.astype(jnp.bfloat16), ("role", "tp")).astype(jnp.float32)
    scale = lax.rsqrt(jnp.mean(stream * stream, axis=1, keepdims=True) + epsilon)
    outgoing = (stream * scale * norm_gain).astype(jnp.bfloat16)
    own_normed = lax.dynamic_slice_in_dim(outgoing, share * quarter, quarter, 1)
    attended = lax.dynamic_slice_in_dim(stream, share * quarter, quarter, 1)
    logits = lax.psum(
        jnp.dot(own_normed, router, preferred_element_type=jnp.float32), ("role", "tp")
    )
    tokens = route_ids.shape[0]
    experts_count = logits.shape[1]
    capacity = max(3, tokens * route_ids.shape[1] // experts_count + 2)
    select, mixing = slot_tables(route_ids, logits, capacity)
    outbound = jnp.einsum(
        "ts,tf->sf", select.astype(jnp.bfloat16), outgoing, preferred_element_type=jnp.float32
    )
    outbound = outbound.astype(jnp.bfloat16).reshape(experts_count, capacity, -1)
    returned = serve(
        lax.all_to_all(outbound, "grp", split_axis=0, concat_axis=0, tiled=True),
        w_gate,
        w_up,
        w_down,
    )
    stacked = returned.reshape(-1, returned.shape[2]).astype(jnp.float32)
    combined = jnp.dot(mixing, stacked, precision=lax.Precision.HIGHEST)
    combined = lax.psum_scatter(
        combined.astype(jnp.bfloat16), ("role", "tp"), scatter_dimension=1, tiled=True
    ).astype(jnp.float32)
    return (attended.astype(jnp.bfloat16), combined.astype(jnp.bfloat16))


def solution(mesh):
    placed = (
        P("grp", ("role", "tp")),
        P("grp", ("role", "tp")),
        P("grp", ("role", "tp")),
        P("grp", None, ("role", "tp")),
        P("grp", None, ("role", "tp")),
        P("grp"),
        P("grp"),
        P("grp", ("role", "tp")),
        P(("role", "tp"), None),
        P(),
        P(("role", "tp"), None),
        P("grp", None),
        P("grp", None, ("role", "tp")),
        P("grp", None, ("role", "tp")),
        P("grp", ("role", "tp"), None),
    )
    return jax.shard_map(
        local,
        mesh=mesh,
        in_specs=placed,
        out_specs=(P("grp", ("role", "tp")), P("grp", ("role", "tp"))),
        check_vma=False,
    )
```

profile of v0, /device:TPU:0, one launch (start us, length us, event | category | flops | bytes accessed | tf_op | source)
XLA Modules:
  0.0 172.5 jit_solution(14774596593833444122)
XLA Ops:
  7.2 0.9 reshape.146
  8.2 0.8 reshape.137
  8.9 1.0 reshape.131
  10.0 0.2 fusion.38
  10.2 0.4 copy-done.2
  10.6 0.1 copy.65
  10.7 1.6 copy.52
  12.3 0.1 fusion.28
  12.4 1.4 fusion.37
  13.8 0.1 copy.53
  13.9 0.1 copy.54
  14.0 0.3 fusion.19
  14.3 0.1 copy.55
  14.3 0.1 copy.56
  14.4 0.7 copy.58
  15.1 1.6 copy.57
  16.8 2.1 %fusion.13 = bf16[32,2,8,64]{3,2,1,0:T(8,128)(2,1)} fusion(bf16[32,128,2,64]{1,3,2,0:T(8,128)(2,1)S(1)} %bitcast.66, f32[32,2,8,128]{3,2,1,0:T(8,128)S(1)} %get-tuple-element.9, f32[32,2,64]{2,1,0:T(2,128)S(1)} %reshape.137, f32[32,2,8]{2,1,0:T(2,128)} %copy.58, f32[32,2,8]{2,1,0:T(2,128)S(1)} %copy.56, f32[32,2,8]{2,1,0:T(2,128)S(1)} %copy.54, ...), kind=kOutput, calls=%fused_computation.15 | convolution fusion | flops 8749056 | bytes 1402880 | tf_op jit(solution)/shard_map/tkgs,tskd->tkgd/dot_general | solution.py:40
  18.9 1.0 convert_element_type.74
  20.0 5.2 %convolution_convert_fusion.2 = bf16[32,2880]{1,0:T(8,128)(2,1)} fusion(bf16[32,1024]{1,0:T(8,128)(2,1)S(1)} %convert_element_type.74, bf16[1024,2880]{0,1:T(8,128)(2,1)} %param.23), kind=kOutput, calls=%fused_computation.4 | convolution fusion | flops 188835840 | bytes 6148096 | tf_op jit(solution)/shard_map/dot_general | solution.py:103
  25.2 0.0 reduce-scatter.4.cloned.1.call-start
  25.3 0.1 copy.59
  25.4 0.1 reduce_window_sum.11
  25.4 0.1 copy.61
  25.6 6.9 %all-gather = bf16[4,720,32]{1,2,0:T(8,128)(2,1)S(1)} all-gather(bf16[1,720,32]{1,2,0:T(8,128)(2,1)S(1)} %bitcast.68), channel_id=1, replica_groups=mesh['role'=2,'grp'=8,'tp'=2] {'role','tp'}, dimensions={0}, use_global_device_ids=true | all-gather | bytes 230400 | tf_op jit(solution)/shard_map/all_gather | solution.py:104
  32.4 0.2 copy.51
  32.6 0.2 reshape.140
  32.9 27.2 %all-reduce.2.cloned.1.call-done = bf16[32,2880]{1,0:T(8,128)(2,1)} async-done(((bf16[32,2880]{1,0:T(8,128)(2,1)}), bf16[32,2880]{1,0:T(8,128)(2,1)}) %all-reduce.2.cloned.1.call-update) | async-done | bytes 184336 | tf_op jit(solution)/shard_map/psum | solution.py:106
  60.0 1.1 multiply_reduce_fusion
  61.1 0.7 copy-done.1
  61.9 0.1 multiply_convert_fusion
  62.0 0.2 fusion.25
  62.2 5.7 %psum.15 = f32[32,8]{0,1:T(8,128)S(1)} all-reduce(f32[32,8]{0,1:T(8,128)S(1)} %fusion.25), channel_id=1, replica_groups=mesh['role'=2,'grp'=8,'tp'=2] {'role','tp'}, use_global_device_ids=true, to_apply=%region_7.8 | all-reduce | flops 256 | bytes 2048 | tf_op jit(solution)/shard_map/psum | solution.py:111
  68.0 0.1 fusion.17
  68.1 0.2 copy.62
  68.2 0.1 convert_element_type.82
  68.4 1.3 convolution_convert_fusion.1
  69.7 1.4 reshape.135
  71.1 33.4 %all_to_all.10 = bf16[8,18,2880]{2,1,0:T(8,128)(2,1)} all-to-all(bf16[8,18,2880]{2,1,0:T(8,128)(2,1)S(1)} %reshape.135), channel_id=1, replica_groups=mesh['role'=2,'grp'=8,'tp'=2] {'grp'}, dimensions={0} | all-to-all | bytes 1658880 | tf_op jit(solution)/shard_map/all_to_all | solution.py:123
  104.6 1.7 reshape.136
  106.3 2.6 %fusion.4 = f32[144,360]{1,0:T(8,128)S(1)} fusion(bf16[144,2880]{1,0:T(8,128)(2,1)S(1)} %reshape.136, bf16[1,2880,360]{1,2,0:T(8,128)(2,1)} %param.27), kind=kOutput, calls=%fused_computation.8 | convolution fusion | flops 298598400 | bytes 3110400 | tf_op jit(solution)/shard_map/dot_general | solution.py:73
  108.9 0.8 fusion.14
  109.8 0.8 convolution_convert_fusion
  110.6 30.5 %all_to_all.11 = bf16[8,18,2880]{2,1,0:T(8,128)(2,1)S(1)} all-to-all(bf16[8,18,2880]{2,1,0:T(8,128)(2,1)S(1)} %convolution_convert_fusion), channel_id=1, replica_groups=mesh['role'=2,'grp'=8,'tp'=2] {'grp'}, dimensions={0} | all-to-all | bytes 1658880 | tf_op jit(solution)/shard_map/all_to_all | solution.py:80
  141.1 0.8 fusion
  141.9 1.2 copy.66
  143.1 1.6 dynamic-slice_convert_fusion
  144.7 19.3 %reduce-scatter.4.cloned.1.call-done = bf16[720,32]{1,0:T(8,128)(2,1)} async-done(((bf16[2880,32]{1,0:T(8,128)(2,1)}), bf16[720,32]{1,0:T(8,128)(2,1)}) %reduce-scatter.4.cloned.1.call-update) | async-done | bytes 46096
  164.0 1.7 copy.67
  (33 shorter events, 0.3 us)
Async XLA Ops:
  7.2 102.6 %copy-start = (bf16[1,360,2880]{2,1,0:T(8,128)(2,1)S(1)}, bf16[1,360,2880]{2,1,0:T(8,128)(2,1)}, u32[]{:S(2)}) copy-start(bf16[1,360,2880]{2,1,0:T(8,128)(2,1)} %param.29) | copy-start | bytes 6220804
  7.2 5.1 %copy-start.8 = (s32[32]{0:T(128)S(1)}, s32[32]{0:T(128)}, u32[]{:S(2)}) copy-start(s32[32]{0:T(128)} %param.21) | copy-start | bytes 388
  7.2 5.1 %copy-start.7 = (s32[32]{0:T(128)S(1)}, s32[32]{0:T(128)}, u32[]{:S(2)}) copy-start(s32[32]{0:T(128)} %param.20) | copy-start | bytes 388
  7.2 52.8 %all-reduce.2.cloned.1.call-start = ((), (), s32[]{:S(2)}) async-start(), calls=%async_computation.3 | async-start | bytes 376832 | tf_op jit(solution)/shard_map/psum | solution.py:106
  10.0 0.6 copy-start.2
  19.9 5.3 %copy-start.4 = (s32[32,4]{0,1:T(4,128)S(1)}, s32[32,4]{0,1:T(4,128)}, u32[]{:S(2)}) copy-start(s32[32,4]{0,1:T(4,128)} %param.26) | copy-start | bytes 1540
  20.0 5.6 %copy-start.3 = (bf16[32,720]{1,0:T(8,128)(2,1)S(1)}, bf16[32,720]{1,0:T(8,128)(2,1)}, u32[]{:S(2)}) copy-start(bf16[32,720]{1,0:T(8,128)(2,1)} %param.22) | copy-start | bytes 138244
  25.2 36.7 %copy-start.6 = (f32[2880]{0:T(1024)S(1)}, f32[2880]{0:T(1024)}, u32[]{:S(2)}) copy-start(f32[2880]{0:T(1024)} %param.24) | copy-start | bytes 34564
  25.2 36.8 %copy-start.5 = (bf16[720,8]{0,1:T(8,128)(2,1)S(1)}, bf16[720,8]{0,1:T(8,128)(2,1)}, u32[]{:S(2)}) copy-start(bf16[720,8]{0,1:T(8,128)(2,1)} %param.25) | copy-start | bytes 34564
  25.2 138.8 %reduce-scatter.4.cloned.1.call-start = ((), (), s32[]{:S(2)}) async-start(), calls=%async_computation.4 | async-start | bytes 921600
  61.1 0.8 copy-start.1
  106.3 2.6 %copy-start.9 = (bf16[1,2880,360]{1,2,0:T(8,128)(2,1)S(1)}, bf16[1,2880,360]{1,2,0:T(8,128)(2,1)}, u32[]{:S(2)}) copy-start(bf16[1,2880,360]{1,2,0:T(8,128)(2,1)} %param.28) | copy-start | bytes 6220804
Sparse Core Ops, SparseCore 0:
  25.3 34.6 all-reduce.1
  143.2 20.7 reduce-scatter.3
where the time goes:
time: 173 us
  blocking collectives  76.6 us (44%)
  waiting for transfers between devices  46.5 us (27%)
  local copies, waits for them, and re-layouts  17.7 us (10%)
  matrix products  15.4 us (9%)
  between operations  14.3 us (8%)
  other arithmetic  1.84 us (1%)
    all_to_all x1, blocking collectives, local(): lax.all_to_all(outbound, 'grp', split_axis=0, concat_axis=0, tiled=True)  33.4 us
    all_to_all x1, blocking collectives, serve(): lax.all_to_all(rounded, 'grp', split_axis=0, concat_axis=0, tiled=True)  30.5 us
    psum x1, waiting for transfers between devices, local(): lax.psum(projected.astype(jnp.bfloat16), ('role', 'tp')).astype(jnp.float32)  27.2 us
    unnamed x3, waiting for transfers between devices  19.3 us
    unnamed x24, local copies, waits for them, and re-layouts  7.26 us
    all_gather x1, blocking collectives, local(): lax.all_gather(residual, ('role', 'tp'), axis=1, tiled=True)  6.87 us
    psum x1, blocking collectives, local(): lax.psum(jnp.dot(own_normed, router, preferred_element_type=jnp.float32),...  5.74 us
    dot_general x1, matrix products, local(): projected = jnp.dot(heads_out, out_proj, preferred_element_type=jnp.float32)  5.22 us
  transfers between devices with their start and end apart: 2, of which 2 were waited for; matrix products, arithmetic and copies ran while one was open for 1% of the time, Pallas kernels for 0%

commit v1 on v0

--- a/solution.py
+++ b/solution.py
@@ -103,7 +103,9 @@
     projected = jnp.dot(heads_out, out_proj, preferred_element_type=jnp.float32)
     stream = lax.all_gather(residual, ("role", "tp"), axis=1, tiled=True).astype(
         jnp.float32
-    ) + lax.psum(projected.astype(jnp.bfloat16), ("role", "tp")).astype(jnp.float32)
+    ) + jnp.sum(lax.all_gather(projected.astype(jnp.bfloat16), ("role", "tp")), axis=0).astype(
+        jnp.float32
+    )
     scale = lax.rsqrt(jnp.mean(stream * stream, axis=1, keepdims=True) + epsilon)
     outgoing = (stream * scale * norm_gain).astype(jnp.bfloat16)
     own_normed = lax.dynamic_slice_in_dim(outgoing, share * quarter, quarter, 1)

time: 173 us -> 162 us (0.936)
  waiting for transfers between devices: 46.5 us -> 19.9 us
  blocking collectives: 76.6 us -> 85.9 us
  other arithmetic: 1.84 us -> 6.06 us
    psum x1 -> x0, waiting for transfers between devices: 27.2 us -> none  [local(): lax.psum(projected.astype(jnp.bfloat16), ('role', 'tp')).astype(jnp.float32)]
    all_gather x0 -> x1, blocking collectives: none -> 8.76 us  [local(): lax.all_gather(projected.astype(jnp.bfloat16), ('role', 'tp'))]
    unnamed x24 -> x28, local copies, waits for them, and re-layouts: 7.26 us -> 6.49 us
    unnamed x3 -> x2, waiting for transfers between devices: 19.3 us -> 19.9 us
  transfers between devices with their start and end apart: 2 -> 1, of which waited for: 2 -> 1; matrix products, arithmetic and copies ran while one was open for 1% -> 1% of each run, Pallas kernels for 0% -> 0%
where the time goes in v1:
time: 162 us; the launch traced here: 161 us
  blocking collectives  85.9 us (53%)
  waiting for transfers between devices  19.9 us (12%)
  local copies, waits for them, and re-layouts  18.8 us (12%)
  matrix products  16.2 us (10%)
  between operations  14.3 us (9%)
  other arithmetic  6.06 us (4%)
    all_to_all x1, blocking collectives, local(): lax.all_to_all(outbound, 'grp', split_axis=0, concat_axis=0, tiled=True)  32.5 us
    all_to_all x1, blocking collectives, serve(): lax.all_to_all(rounded, 'grp', split_axis=0, concat_axis=0, tiled=True)  30.4 us
    unnamed x2, waiting for transfers between devices  19.9 us
    all_gather x1, blocking collectives, local(): lax.all_gather(projected.astype(jnp.bfloat16), ('role', 'tp'))  8.76 us
    psum x1, blocking collectives, local(): lax.psum(jnp.dot(own_normed, router, preferred_element_type=jnp.float32),...  7.18 us
    all_gather x1, blocking collectives, local(): lax.all_gather(residual, ('role', 'tp'), axis=1, tiled=True)  7.06 us
    unnamed x28, local copies, waits for them, and re-layouts  6.49 us
    dot_general x1, matrix products, local(): projected = jnp.dot(heads_out, out_proj, preferred_element_type=jnp.float32)  4.51 us
  transfers between devices with their start and end apart: 1, of which 1 were waited for; matrix products, arithmetic and copies ran while one was open for 1% of the time, Pallas kernels for 0%

profile of v1, /device:TPU:0, one launch (start us, length us, event | category | flops | bytes accessed | tf_op | source)
XLA Modules:
  0.0 161.2 jit_solution(11152564190663925649)
XLA Ops:
  7.2 0.8 convert_reduce_fusion
  8.1 1.3 iota_compare_fusion.1
  9.3 0.1 copy.63
  9.5 0.7 select_reduce_fusion.1
  10.2 0.6 iota_compare_fusion
  10.9 0.8 reshape.147
  11.6 1.4 reshape.137
  13.0 1.0 reshape.131
  14.1 0.2 fusion.38
  14.2 0.1 copy.69
  14.3 0.4 copy-done.2
  14.7 7.1 %all-gather.1 = bf16[4,720,32]{1,2,0:T(8,128)(2,1)S(1)} all-gather(bf16[1,720,32]{1,2,0:T(8,128)(2,1)} %bitcast.70), channel_id=1, replica_groups=mesh['role'=2,'grp'=8,'tp'=2] {'role','tp'}, dimensions={0}, use_global_device_ids=true | all-gather | bytes 230400 | tf_op jit(solution)/shard_map/all_gather | solution.py:104
  21.8 0.2 copy.55
  21.9 0.2 reshape.141
  22.2 1.6 %copy.56 = bf16[32,128,128]{1,2,0:T(8,128)(2,1)S(1)} copy(bf16[32,128,128]{2,1,0:T(8,128)(2,1)} %param.18) | data formatting | bytes 2097152 | tf_op args[3]
  23.8 0.8 fusion.28
  24.6 2.6 %fusion.37 = (f32[32,2,8]{2,1,0:T(2,128)}, f32[32,2,8,128]{3,2,1,0:T(8,128)}) fusion(bf16[32,2,8,64]{3,2,1,0:T(8,128)(2,1)} %copy-done.2, bf16[32,128,2,64]{1,3,2,0:T(8,128)(2,1)S(1)} %bitcast.65, pred[32,128]{1,0:T(8,128)(4,1)S(1)} %fusion.28), kind=kOutput, calls=%fused_computation.59 | convolution fusion | flops 8584704 | bytes 1382400 | tf_op jit(solution)/shard_map/tkgd,tskd->tkgs/dot_general | solution.py:24
  27.2 0.8 copy.57
  28.0 0.1 copy.58
  28.1 1.2 fusion.19
  29.5 0.7 copy.60
  30.1 0.7 copy.62
  30.8 1.6 %copy.61 = bf16[32,128,128]{1,2,0:T(8,128)(2,1)S(1)} copy(bf16[32,128,128]{2,1,0:T(8,128)(2,1)} %param.19) | data formatting | bytes 2097152 | tf_op args[4]
  32.5 2.4 %fusion.13 = bf16[32,2,8,64]{3,2,1,0:T(8,128)(2,1)} fusion(bf16[32,128,2,64]{1,3,2,0:T(8,128)(2,1)S(1)} %bitcast.68, f32[32,2,8,128]{3,2,1,0:T(8,128)} %get-tuple-element.9, f32[32,2,64]{2,1,0:T(2,128)} %reshape.137, f32[32,2,8]{2,1,0:T(2,128)} %copy.62, f32[32,2,8]{2,1,0:T(2,128)} %copy.60, f32[32,2,8]{2,1,0:T(2,128)} %copy-done.3, ...), kind=kOutput, calls=%fused_computation.15 | convolution fusion | flops 8749056 | bytes 1402880 | tf_op jit(solution)/shard_map/tkgs,tskd->tkgd/dot_general | solution.py:40
  34.9 1.0 convert_element_type.76
  35.9 4.5 %convolution_convert_fusion.2 = bf16[32,2880]{1,0:T(8,128)(2,1)S(1)} fusion(bf16[32,1024]{1,0:T(8,128)(2,1)S(1)} %convert_element_type.76, bf16[1024,2880]{0,1:T(8,128)(2,1)} %param.23), kind=kOutput, calls=%fused_computation.4 | convolution fusion | flops 188835840 | bytes 6148096 | tf_op jit(solution)/shard_map/dot_general | solution.py:103
  40.5 8.8 %all-gather = bf16[128,2880]{1,0:T(8,128)(2,1)S(1)} all-gather(bf16[32,2880]{1,0:T(8,128)(2,1)S(1)} %convolution_convert_fusion.2), channel_id=2, replica_groups=mesh['role'=2,'grp'=8,'tp'=2] {'role','tp'}, dimensions={0}, use_global_device_ids=true | all-gather | bytes 921600 | tf_op jit(solution)/shard_map/all_gather | solution.py:106
  49.2 0.1 reduce_sum.85
  49.4 0.2 multiply_reduce_fusion
  49.6 0.1 multiply_convert_fusion
  49.7 0.2 fusion.25
  49.9 7.2 %psum.7 = f32[32,8]{0,1:T(8,128)S(1)} all-reduce(f32[32,8]{0,1:T(8,128)S(1)} %fusion.25), channel_id=1, replica_groups=mesh['role'=2,'grp'=8,'tp'=2] {'role','tp'}, use_global_device_ids=true, to_apply=%region_7.8 | all-reduce | flops 256 | bytes 2048 | tf_op jit(solution)/shard_map/psum | solution.py:113
  57.1 0.1 fusion.17
  57.2 0.2 copy.66
  57.4 0.1 convert_element_type.84
  57.5 1.3 convolution_convert_fusion.1
  58.8 1.4 reshape.135
  60.3 32.5 %all_to_all.10 = bf16[8,18,2880]{2,1,0:T(8,128)(2,1)} all-to-all(bf16[8,18,2880]{2,1,0:T(8,128)(2,1)S(1)} %reshape.135), channel_id=1, replica_groups=mesh['role'=2,'grp'=8,'tp'=2] {'grp'}, dimensions={0} | all-to-all | bytes 1658880 | tf_op jit(solution)/shard_map/all_to_all | solution.py:125
  92.8 1.7 %reshape.136 = bf16[144,2880]{1,0:T(8,128)(2,1)S(1)} reshape(bf16[8,18,2880]{2,1,0:T(8,128)(2,1)} %all_to_all.10) | data formatting | bytes 1658880 | tf_op jit(solution)/shard_map/reshape | solution.py:72
  94.5 2.6 %fusion.4 = f32[144,360]{1,0:T(8,128)S(1)} fusion(bf16[144,2880]{1,0:T(8,128)(2,1)S(1)} %reshape.136, bf16[1,2880,360]{1,2,0:T(8,128)(2,1)} %param.27), kind=kOutput, calls=%fused_computation.8 | convolution fusion | flops 298598400 | bytes 3110400 | tf_op jit(solution)/shard_map/dot_general | solution.py:73
  97.1 0.8 fusion.14
  98.0 0.8 convolution_convert_fusion
  98.8 30.4 %all_to_all.11 = bf16[8,18,2880]{2,1,0:T(8,128)(2,1)S(1)} all-to-all(bf16[8,18,2880]{2,1,0:T(8,128)(2,1)S(1)} %convolution_convert_fusion), channel_id=1, replica_groups=mesh['role'=2,'grp'=8,'tp'=2] {'grp'}, dimensions={0} | all-to-all | bytes 1658880 | tf_op jit(solution)/shard_map/all_to_all | solution.py:80
  129.2 0.8 fusion
  130.0 1.2 copy.70
  131.2 1.6 %dynamic-slice_convert_fusion = bf16[32,720]{1,0:T(8,128)(2,1)} fusion(f32[32,2880]{1,0:T(8,128)} %copy-done.1, s32[]{:T(128)S(6)} %select_n.37), kind=kLoop, calls=%fused_computation.32 | loop fusion | bytes 92164 | tf_op jit(solution)/shard_map/convert_element_type | solution.py:135
  132.8 19.9 %reduce-scatter.4.cloned.1.call-done = bf16[720,32]{1,0:T(8,128)(2,1)} async-done(((bf16[2880,32]{1,0:T(8,128)(2,1)}), bf16[720,32]{1,0:T(8,128)(2,1)}) %reduce-scatter.4.cloned.1.call-update) | async-done | bytes 46096
  152.7 1.7 %copy.71 = bf16[32,720]{1,0:T(8,128)(2,1)} copy(bf16[32,720]{0,1:T(8,128)(2,1)} %bitcast.69) | data formatting | bytes 92160
  (36 shorter events, 0.5 us)
Async XLA Ops:
  7.2 90.8 %copy-start = (bf16[1,360,2880]{2,1,0:T(8,128)(2,1)S(1)}, bf16[1,360,2880]{2,1,0:T(8,128)(2,1)}, u32[]{:S(2)}) copy-start(bf16[1,360,2880]{2,1,0:T(8,128)(2,1)} %param.29) | copy-start | bytes 6220804
  7.2 145.6 %reduce-scatter.4.cloned.1.call-start = ((), (), s32[]{:S(2)}) async-start(), calls=%async_computation.3 | async-start | bytes 921600
  14.0 0.7 copy-start.2
  24.6 2.6 %copy-start.5 = (pred[32,128]{1,0:T(8,128)(4,1)}, pred[32,128]{1,0:T(8,128)(4,1)S(1)}, u32[]{:S(2)}) copy-start(pred[32,128]{1,0:T(8,128)(4,1)S(1)} %fusion.28) | copy-start | bytes 12292
  28.1 2.0 %copy-start.3 = (f32[32,2,8]{2,1,0:T(2,128)}, f32[32,2,8]{2,1,0:T(2,128)S(1)}, u32[]{:S(2)}) copy-start(f32[32,2,8]{2,1,0:T(2,128)S(1)} %copy.58) | copy-start | bytes 6148
  29.4 3.0 %copy-start.6 = (pred[32,128]{1,0:T(8,128)(4,1)S(1)}, pred[32,128]{1,0:T(8,128)(4,1)}, u32[]{:S(2)}) copy-start(pred[32,128]{1,0:T(8,128)(4,1)} %copy-done.5) | copy-start | bytes 12292
  40.4 9.2 %copy-start.10 = (f32[2880]{0:T(1024)S(1)}, f32[2880]{0:T(1024)}, u32[]{:S(2)}) copy-start(f32[2880]{0:T(1024)} %param.24) | copy-start | bytes 34564
  40.4 9.3 %copy-start.9 = (bf16[720,8]{0,1:T(8,128)(2,1)S(1)}, bf16[720,8]{0,1:T(8,128)(2,1)}, u32[]{:S(2)}) copy-start(bf16[720,8]{0,1:T(8,128)(2,1)} %param.25) | copy-start | bytes 34564
  40.4 16.6 %copy-start.7 = (s32[32,4]{0,1:T(4,128)S(1)}, s32[32,4]{0,1:T(4,128)}, u32[]{:S(2)}) copy-start(s32[32,4]{0,1:T(4,128)} %param.26) | copy-start | bytes 1540
  40.5 16.7 %copy-start.4 = (pred[32,4,18]{0,2,1:T(8,128)(4,1)S(1)}, pred[32,4,18]{0,2,1:T(8,128)(4,1)}, u32[]{:S(2)}) copy-start(pred[32,4,18]{0,2,1:T(8,128)(4,1)} %iota_compare_fusion) | copy-start | bytes 6916
  40.5 16.7 %copy-start.8 = (pred[32,4,8]{0,2,1:T(8,128)(4,1)S(1)}, pred[32,4,8]{0,2,1:T(8,128)(4,1)}, u32[]{:S(2)}) copy-start(pred[32,4,8]{0,2,1:T(8,128)(4,1)} %iota_compare_fusion.1) | copy-start | bytes 3076
  49.5 8.0 %copy-start.1 = (f32[32,2880]{1,0:T(8,128)}, f32[32,2880]{1,0:T(8,128)S(1)}, u32[]{:S(2)}) copy-start(f32[32,2880]{1,0:T(8,128)S(1)} %get-tuple-element.5) | copy-start | bytes 1105924
  94.5 2.6 %copy-start.11 = (bf16[1,2880,360]{1,2,0:T(8,128)(2,1)S(1)}, bf16[1,2880,360]{1,2,0:T(8,128)(2,1)}, u32[]{:S(2)}) copy-start(bf16[1,2880,360]{1,2,0:T(8,128)(2,1)} %param.28) | copy-start | bytes 6220804
Sparse Core Ops, SparseCore 0:
  131.3 21.3 reduce-scatter.3
